TPU v7x, 32 devices: a 4x4x1 block of a 4x4x8 slice. The times are simulated.
32 devices in a mesh: part: 1 (over z), data: 4 (over y), seq: 8 (over x, core).
Axes of the slice: x: 4, y: 4, z: 1, core: 2. Of those that a mesh axis runs over, the one named last changes fastest.
The devices are a block of a 4x4x8 slice.
Arguments:
- enc_out: bfloat16 [128, 64, 512], P(('part', 'data'), 'seq')
- pred_out: bfloat16 [128, 32, 512], P(('part', 'data'))
- w_enc: bfloat16 [512, 640], replicated
- w_pred: bfloat16 [512, 640], replicated
- w_out: bfloat16 [640, 1024], replicated
- labels: int32 [128, 31], P(('part', 'data'))
- frame_len: int32 [128], P(('part', 'data'))
- label_len: int32 [128], P(('part', 'data'))
Outputs:
- output 1: float32 [128], P(('part', 'data'))
- output 2: bfloat16 [128, 64, 512], P(('part', 'data'), 'seq')
- output 3: float32 [128, 32, 512], P(('part', 'data'))
- output 4: float32 [512, 640], P('part')
- output 5: float32 [512, 640], P('part')
- output 6: float32 [640, 1024], P('part')
All inputs are finite; a program needn't handle non-finite values.
Results may differ from a plain program's by a relative error of at most 0.0127134.
Values are sent between devices in bfloat16 or wider.
A program may use at most 768 MiB of HBM per device.

v0:
```python
import functools

import jax
import jax.numpy as jnp
from jax import lax
from jax.experimental import pallas as pl
from jax.experimental.pallas import tpu as pltpu
from jax.sharding import PartitionSpec as P

NEG = -1e30
MESH = pl.DeviceIdType.MESH
VMEM = pltpu.VMEM
F32 = jnp.float32
BF16 = jnp.bfloat16
VMEM_LIMIT = 67_000_000
SUB = 8
LANES = 128
GROUPS = 4
WIDE = 8
BLOCK = 32
CORES = 2
RING = 4


def vspec():
    return pl.BlockSpec(memory_space=pltpu.VMEM)


def in_hbm(x):
    return pltpu.with_memory_space_constraint(x, pltpu.HBM)


def in_vmem(x):
    return pltpu.with_memory_space_constraint(x, pltpu.VMEM)


def sspec():
    return pl.BlockSpec(memory_space=pltpu.SMEM)


def exchange_kernel(n_seq, flen_hbm, llen_hbm, enc_hbm, pred_hbm, w_enc_hbm, w_pred_hbm, w_out_hbm,
                    order_ref, place_ref, frames_ref, a_ref, c_ref, w_out_t_ref,
                    key_ref, sorted_ref, own_pred_ref, flen_ref, llen_ref, enc_ref, pred_ref, w_enc_ref, w_pred_ref, w_out_ref, load_sem, send_sem, recv_sem):
    sources = (flen_hbm, llen_hbm, enc_hbm, pred_hbm, w_pred_hbm, w_out_hbm, w_enc_hbm)
    landed = (flen_ref, llen_ref, enc_ref, pred_ref, w_pred_ref, w_out_ref, w_enc_ref)
    loads = [pltpu.make_async_copy(src, dst, load_sem.at[k]) for k, (src, dst) in enumerate(zip(sources, landed))]
    for copy in loads:
        copy.start()
    seq = lax.axis_index("seq")
    n_utt = enc_ref.shape[0]
    n_own = n_utt // n_seq
    barrier = pltpu.get_barrier_semaphore()
    for hop in range(1, n_seq):
        pl.semaphore_signal(barrier, inc=1, device_id={"seq": lax.rem(seq + hop, n_seq)}, device_id_type=MESH)

    def set_key(i, carry):
        key_ref[i] = ((flen_ref[i] + SUB - 1) // SUB) * ((llen_ref[i] + SUB) // SUB) * n_utt + i
        return carry

    def set_place(i, carry):
        key = key_ref[i]
        rank = jnp.int32(0)
        for j in range(n_utt):
            rank = rank + jnp.where(key_ref[j] > key, 1, 0)
        deal = rank // n_seq
        at = rank - deal * n_seq
        at = jnp.where(deal % 2 == 0, at, n_seq - 1 - at)
        place_ref[i] = at * n_own + deal
        return carry

    def set_order(k, carry):
        utt = jnp.int32(0)
        for j in range(n_utt):
            utt = utt + jnp.where(place_ref[j] == k, j, 0)
        order_ref[k] = utt
        return carry

    loads[0].wait()
    loads[1].wait()
    lax.fori_loop(0, n_utt, set_key, 0)
    lax.fori_loop(0, n_utt, set_place, 0)
    lax.fori_loop(0, n_utt, set_order, 0)
    loads[2].wait()
    for k in range(n_utt):
        sorted_ref[k] = enc_ref[order_ref[k]]
    pl.semaphore_wait(barrier, n_seq - 1)
    copies = []
    for hop in range(1, n_seq):
        peer = lax.rem(seq + hop, n_seq)
        copy = pltpu.make_async_remote_copy(
            src_ref=sorted_ref.at[pl.ds(peer * n_own, n_own)],
            dst_ref=frames_ref.at[seq],
            send_sem=send_sem.at[hop - 1],
            recv_sem=recv_sem.at[hop - 1],
            device_id={"seq": peer},
            device_id_type=MESH,
        )
        copy.start()
        copies.append(copy)
    frames_ref[pl.ds(seq, 1)] = sorted_ref[pl.ds(seq * n_own, n_own)][None]
    loads[3].wait()
    loads[4].wait()
    for j in range(n_own):
        own_pred_ref[j] = pred_ref[order_ref[seq * n_own + j]]
    own_pred = own_pred_ref[...]
    c_ref[...] = jnp.dot(own_pred.reshape(-1, own_pred.shape[-1]), w_pred_ref[...], preferred_element_type=F32).astype(BF16).astype(F32)
    loads[5].wait()
    w_out_t_ref[...] = w_out_ref[...].T
    loads[6].wait()
    for copy in copies:
        copy.wait()
    frames = frames_ref[...]
    a_ref[...] = jnp.dot(frames.reshape(-1, frames.shape[-1]), w_enc_ref[...], preferred_element_type=F32).astype(BF16).astype(F32)


def exchange(n_seq, frame_len, label_len, enc_loc, pred_loc, w_enc, w_pred, w_out):
    n_utt, t_loc, width = enc_loc.shape
    n_own = n_utt // n_seq
    n_upos = pred_loc.shape[1]
    joint, vocab = w_out.shape
    return pl.pallas_call(
        functools.partial(exchange_kernel, n_seq),
        out_shape=(
            pltpu.HBM((n_utt,), jnp.int32),
            pltpu.HBM((n_utt,), jnp.int32),
            pltpu.HBM((n_seq, n_own, t_loc, width), BF16),
            VMEM((n_seq * n_own * t_loc, joint), F32),
            VMEM((n_own * n_upos, joint), F32),
            VMEM((vocab, joint), BF16),
        ),
        in_specs=[pl.BlockSpec(memory_space=pltpu.HBM)] * 7,
        out_specs=(sspec(),) * 2 + (vspec(),) * 4,
        scratch_shapes=[
            pltpu.SMEM((n_utt,), jnp.int32),
            VMEM(enc_loc.shape, BF16),
            VMEM((n_own, n_upos, width), BF16),
            pltpu.SMEM((n_utt,), jnp.int32),
            pltpu.SMEM((n_utt,), jnp.int32),
        ]
        + [VMEM(v.shape, BF16) for v in (enc_loc, pred_loc, w_enc, w_pred, w_out)]
        + [
            pltpu.SemaphoreType.DMA((7,)),
            pltpu.SemaphoreType.DMA((n_seq - 1,)),
            pltpu.SemaphoreType.DMA((n_seq - 1,)),
        ],
        compiler_params=pltpu.CompilerParams(collective_id=0, has_side_effects=True, vmem_limit_bytes=40_000_000),
        name="exchange",
    )(*(in_hbm(v) for v in (frame_len, label_len, enc_loc, pred_loc, w_enc, w_pred, w_out)))


def logaddexp(x, y):
    top = jnp.maximum(x, y)
    return top + jnp.log(1.0 + jnp.exp(-jnp.abs(x - y)))


def lattice_kernel(n_own, n_frames, n_upos, seq_ref, order_ref, flen_ref, llen_ref, labels_ref, a_ref, c_ref, w_ref, wt_ref,
                   da_ref, dc_ref, gw_ref, loss_ref,
                   e_ref, h_ref, blank_ref, label_ref, alpha_ref, beta_ref, ids_ref, dact_ref, dpred_ref, work0, work1, dz_ref, dh_ref):
    vocab = w_ref.shape[1]
    joint = w_ref.shape[0]
    n_vt = vocab // LANES
    rows_g = SUB * SUB
    rows_t = GROUPS * rows_g
    n_diag = n_frames + n_upos - 1
    first = seq_ref[0] * n_own
    utts = [order_ref[first + b] for b in range(n_own)]
    lens_t = [flen_ref[utt] for utt in utts]
    lens_u = [llen_ref[utt] for utt in utts]
    blocks_t = [lax.div(n + SUB - 1, SUB) for n in lens_t]
    blocks_u = [lax.div(n + SUB, SUB) for n in lens_u]
    starts = [jnp.int32(0)]
    for b in range(n_own):
        starts.append(starts[-1] + blocks_t[b] * blocks_u[b])
    total = starts[-1]
    n_tiles = lax.div(total + GROUPS - 1, GROUPS)

    def decode(n):
        n = jnp.minimum(n, total - 1)
        b = jnp.int32(0)
        base, width = starts[0], blocks_u[0]
        for k in range(1, n_own):
            past = n >= starts[k]
            b = jnp.where(past, k, b)
            base = jnp.where(past, starts[k], base)
            width = jnp.where(past, blocks_u[k], width)
        ti = lax.div(n - base, width)
        return n, b, ti, n - base - ti * width

    pos_col = lax.broadcasted_iota(jnp.int32, (n_upos, n_upos - 1), 0)
    pos_row = lax.broadcasted_iota(jnp.int32, (n_upos, n_upos - 1), 1)
    for b in range(n_own):
        row = labels_ref[pl.ds(utts[b], 1), :].astype(F32)
        col = jnp.sum(jnp.where(pos_col == pos_row, row, 0.0), axis=1, keepdims=True)
        ids_ref[pl.ds(b * n_upos, n_upos), :] = jnp.broadcast_to(col, (n_upos, LANES)).astype(jnp.int32)

    blank_ref[...] = jnp.zeros_like(blank_ref)
    label_ref[...] = jnp.zeros_like(label_ref)
    gw_ref[...] = jnp.zeros_like(gw_ref)
    dact_ref[...] = jnp.zeros_like(dact_ref)
    dpred_ref[...] = jnp.zeros_like(dpred_ref)

    lane = lax.broadcasted_iota(jnp.int32, (SUB, LANES), 1)
    block_lane = lax.broadcasted_iota(jnp.int32, (BLOCK, LANES), 1)
    t_block = BLOCK // SUB
    works = (work0, work1)

    def tile_rows(i):
        return pl.ds(pl.multiple_of(jnp.clip(i, 0, n_tiles - 1) * rows_t, rows_t), rows_t)

    def tile_groups(i):
        return [decode(jnp.clip(i, 0, n_tiles - 1) * GROUPS + g) for g in range(GROUPS)]

    def pred_row(b, ui):
        return pl.ds(pl.multiple_of(b * n_upos + ui * SUB, SUB), SUB)

    def act_row(b, ti):
        return pl.ds(pl.multiple_of((ti * n_own + b) * SUB, SUB), SUB)

    def block_ids(b, ui):
        ids = ids_ref[pred_row(b, ui), :]
        return jnp.broadcast_to(ids[None], (t_block, SUB, LANES)).reshape(BLOCK, LANES)

    def cell_rows(ti, k, ui):
        return pl.ds(pl.multiple_of((n_diag - 1 - ti * SUB - k) * n_upos + ui * SUB, SUB), SUB)

    def make_hidden(i):
        first_row = jnp.clip(i, 0, n_tiles - 1) * rows_t
        for g, (n, b, ti, ui) in enumerate(tile_groups(i)):
            a8 = a_ref[act_row(b, ti), :]
            c8 = c_ref[pred_row(b, ui), :]
            h = jnp.tanh(a8[:, None, :] + c8[None, :, :]).reshape(rows_g, joint).astype(BF16)
            h_ref[pl.ds(pl.multiple_of(first_row + g * rows_g, rows_g), rows_g), :] = h

    def make_logits(i, z_ref):
        z_ref[...] = jnp.dot(h_ref[tile_rows(i), :], w_ref[...], preferred_element_type=F32)

    def make_softmax(i, z_ref):
        first_row = jnp.clip(i, 0, n_tiles - 1) * rows_t
        for g, (n, b, ti, ui) in enumerate(tile_groups(i)):
            ids = block_ids(b, ui)
            for r in range(0, rows_g, BLOCK):
                z = z_ref[g * rows_g + r:g * rows_g + r + BLOCK, :]
                top = jnp.max(z, axis=1, keepdims=True)
                e = jnp.exp(z - top)
                norm = jnp.sum(e, axis=1, keepdims=True)
                e_ref[pl.ds(pl.multiple_of(first_row + g * rows_g + r, BLOCK), BLOCK), :] = e
                log_norm = top + jnp.log(norm)
                picked = jnp.zeros((BLOCK, LANES), F32)
                for v in range(n_vt):
                    picked = picked + jnp.where(block_lane + v * LANES == ids, z[:, v * LANES:(v + 1) * LANES], 0.0)
                label = jnp.sum(picked, axis=1, keepdims=True) - log_norm
                blank = z[:, 0:1] - log_norm
                scale = 1.0 / norm
                rows = [cell_rows(ti, r // SUB + k, ui) for k in range(t_block)]
                old_blank = [blank_ref[at, :] for at in rows]
                old_label = [label_ref[at, :] for at in rows]
                for k, at in enumerate(rows):
                    sl = slice(k * SUB, (k + 1) * SUB)
                    blank_ref[at, :] = jnp.where(lane == b, blank[sl], jnp.where(lane == b + n_own, scale[sl], old_blank[k]))
                    label_ref[at, :] = jnp.where(lane == b, label[sl], old_label[k])

    make_hidden(0)
    make_logits(0, work0)
    make_hidden(1)

    def forward(j, carry):
        for half in range(2):
            i = 2 * j + half
            make_logits(i + 1, works[1 - half])
            make_softmax(i, works[half])
            make_hidden(i + 2)
        return carry

    lax.fori_loop(0, lax.div(n_tiles + 1, 2), forward, 0)

    upos = lax.broadcasted_iota(jnp.int32, (n_upos, LANES), 0)
    utt = lax.broadcasted_iota(jnp.int32, (n_upos, LANES), 1)
    t_end = jnp.ones((n_upos, LANES), jnp.int32)
    u_end = jnp.zeros((n_upos, LANES), jnp.int32)
    for b in range(n_own):
        t_end = jnp.where(utt == b, lens_t[b], t_end)
        u_end = jnp.where(utt == b, lens_u[b], u_end)

    def diagonal(d):
        return pl.ds((n_diag - 1 - d) * n_upos, n_upos, stride=n_upos + 1)

    def down(x):
        return jnp.where(upos == 0, NEG, pltpu.roll(x, 1, 0))

    def up(x):
        return jnp.where(upos == n_upos - 1, NEG, pltpu.roll(x, n_upos - 1, 0))

    def edge(d):
        return jnp.where((d - upos == t_end) & (upos == u_end), 0.0, NEG)

    last = functools.reduce(jnp.maximum, [t + u for t, u in zip(lens_t, lens_u)])
    reach = functools.reduce(jnp.maximum, [(t + u) * SUB - 1 for t, u in zip(blocks_t, blocks_u)])
    alpha0 = jnp.where(upos == 0, 0.0, NEG).astype(F32)
    beta0 = edge(last)
    alpha_ref[0] = alpha0
    beta_ref[last] = beta0

    def sweep(k, carry):
        alpha, beta = carry
        d = k + 1
        alpha = logaddexp(alpha + blank_ref[diagonal(k), :], down(alpha + label_ref[diagonal(k), :]))
        alpha = jnp.where(upos <= d, alpha, NEG)
        alpha_ref[d] = alpha
        d = last - 1 - k
        inside = (d - upos < t_end) & (upos <= u_end)
        beta = logaddexp(beta + blank_ref[diagonal(d), :], up(beta) + label_ref[diagonal(d), :])
        beta = jnp.where(inside, beta, edge(d))
        beta_ref[d] = beta
        return alpha, beta

    lax.fori_loop(0, last, sweep, (alpha0, beta0))
    log_prob = beta_ref[0][0:1, :]
    loss_ref[...] = jnp.broadcast_to(-log_prob, (SUB, LANES))

    def occupancy(d, carry):
        t = d - upos
        alpha = alpha_ref[d]
        after = beta_ref[d + 1]
        cell_ok = (t >= 0) & (t < t_end) & (upos <= u_end)
        blank = blank_ref[diagonal(d), :]
        q0 = jnp.where(cell_ok, jnp.exp(alpha + blank + after - log_prob), 0.0)
        q1 = jnp.where(cell_ok & (upos < u_end), jnp.exp(alpha + label_ref[diagonal(d), :] + up(after) - log_prob), 0.0)
        blank_ref[diagonal(d), :] = jnp.where(utt < n_own, q0, blank)
        label_ref[diagonal(d), :] = q1
        return carry

    lax.fori_loop(0, jnp.minimum(reach, n_diag), occupancy, 0)

    sub_row = lax.broadcasted_iota(jnp.int32, (SUB, LANES), 0)

    def group_rows(n, r, size):
        return pl.ds(pl.multiple_of(n * rows_g + r, size), size)

    def make_dz(index, g, n, b, ti, ui):
        keep = (lane == b) & (index < total)
        ids = block_ids(b, ui)
        for r in range(0, rows_g, BLOCK):
            q0s, q1s, scales = [], [], []
            for k in range(t_block):
                at = cell_rows(ti, r // SUB + k, ui)
                blank = blank_ref[at, :]
                q0s.append(jnp.where(keep, blank, 0.0))
                scales.append(jnp.where(lane == b + n_own, blank, 0.0))
                q1s.append(jnp.where(keep, label_ref[at, :], 0.0))
            q0 = jnp.sum(jnp.concatenate(q0s, axis=0), axis=1, keepdims=True)
            q1 = jnp.sum(jnp.concatenate(q1s, axis=0), axis=1, keepdims=True)
            scale = jnp.sum(jnp.concatenate(scales, axis=0), axis=1, keepdims=True) * (q0 + q1)
            for v in range(n_vt):
                cols = slice(v * LANES, (v + 1) * LANES)
                dz = e_ref[group_rows(n, r, BLOCK), cols] * scale
                if v == 0:
                    dz = dz - jnp.where(block_lane == 0, q0, 0.0)
                dz = dz - jnp.where(block_lane + v * LANES == ids, q1, 0.0)
                dz_ref[g * rows_g + r:g * rows_g + r + BLOCK, cols] = dz.astype(BF16)

    def make_sums(g, n, b, ti, ui):
        for v in range(joint // LANES):
            cols = slice(v * LANES, (v + 1) * LANES)
            h = h_ref[group_rows(n, 0, rows_g), cols].astype(F32)
            ds = dh_ref[g * rows_g:(g + 1) * rows_g, cols] * (1.0 - h * h)
            cube = [ds[k * SUB:(k + 1) * SUB] for k in range(SUB)]
            dpred_ref[pred_row(b, ui), cols] += ((cube[0] + cube[1]) + (cube[2] + cube[3])) + ((cube[4] + cube[5]) + (cube[6] + cube[7]))
            for shift in (4, 2, 1):
                low = sub_row % (2 * shift) < shift
                half = len(cube) // 2
                cube = [jnp.where(low, cube[k], cube[k + half]) + jnp.where(low, pltpu.roll(cube[k], SUB - shift, 0), pltpu.roll(cube[k + half], shift, 0)) for k in range(half)]
            dact_ref[act_row(b, ti), cols] += cube[0]

    wide_rows = WIDE * rows_g
    n_wide = lax.div(total + WIDE - 1, WIDE)

    def clear(i, carry):
        h_ref[pl.ds(pl.multiple_of(i * rows_t, rows_t), rows_t), :] = jnp.zeros((rows_t, joint), BF16)
        return carry

    lax.fori_loop(n_tiles, n_wide * (WIDE // GROUPS), clear, 0)

    def backward(i, carry):
        groups = [(i * WIDE + g, g, *decode(i * WIDE + g)) for g in range(WIDE)]
        for group in groups:
            make_dz(*group)
        dh_ref[...] = jnp.dot(dz_ref[...], wt_ref[...], preferred_element_type=F32)
        h = h_ref[pl.ds(pl.multiple_of(i * wide_rows, wide_rows), wide_rows), :]
        for v in range(0, n_vt, 2):
            part = lax.dot_general(h, dz_ref[:, v * LANES:(v + 2) * LANES], (((0,), (0,)), ((), ())), preferred_element_type=F32)
            gw_ref[v] += part[:, :LANES]
            gw_ref[v + 1] += part[:, LANES:]
        for group in groups:
            make_sums(*group[1:])
        return carry

    lax.fori_loop(0, n_wide, backward, 0)
    da_ref[...] = dact_ref[...].astype(BF16)
    dc_ref[...] = dpred_ref[...].astype(BF16)


def lattice(n_seq, seq_idx, order, frame_len, label_len, labels, act, pred, w_out, w_out_t, n_upos, t_loc):
    n_own = frame_len.shape[0] // n_seq
    n_frames = n_seq * t_loc
    joint, vocab = w_out.shape
    cells = n_own * n_frames * n_upos
    n_diag = n_frames + n_upos - 1
    lat_rows = (n_diag + n_upos - 1) * n_upos
    return pl.pallas_call(
        functools.partial(lattice_kernel, n_own, n_frames, n_upos),
        out_shape=(
            VMEM(act.shape, BF16),
            VMEM(pred.shape, BF16),
            VMEM((vocab // LANES, joint, LANES), F32),
            VMEM((SUB, LANES), F32),
        ),
        in_specs=[sspec()] * 4 + [vspec()] * 5,
        out_specs=(vspec(),) * 4,
        scratch_shapes=[
            VMEM((cells, vocab), F32),
            VMEM((cells, joint), BF16),
            VMEM((lat_rows, LANES), F32),
            VMEM((lat_rows, LANES), F32),
            VMEM((n_diag + 1, n_upos, LANES), F32),
            VMEM((n_diag + 1, n_upos, LANES), F32),
            VMEM((n_own * n_upos, LANES), jnp.int32),
            VMEM(act.shape, F32),
            VMEM(pred.shape, F32),
            VMEM((GROUPS * SUB * SUB, vocab), F32),
            VMEM((GROUPS * SUB * SUB, vocab), F32),
            VMEM((WIDE * SUB * SUB, vocab), BF16),
            VMEM((WIDE * SUB * SUB, joint), F32),
        ],
        compiler_params=pltpu.CompilerParams(vmem_limit_bytes=60_400_000),
        name="lattice",
    )(seq_idx, order, frame_len, label_len, labels, in_vmem(act), in_vmem(pred), w_out, in_vmem(w_out_t))


class Copies:
    def __init__(self, send_sem, recv_sem):
        self.sems = (send_sem, recv_sem)
        self.all = []

    def start(self, src, dst, device):
        k = len(self.all)
        copy = pltpu.make_async_remote_copy(src_ref=src, dst_ref=dst, send_sem=self.sems[0].at[k], recv_sem=self.sems[1].at[k], device_id=device, device_id_type=MESH)
        copy.start()
        self.all.append(copy)
        return copy

    def drain(self):
        for copy in self.all:
            copy.wait_send()


class Ring:
    def __init__(self, me, device):
        self.me = me
        self.right, self.left, self.across = [device(lax.rem(me + hop, RING)) for hop in (1, RING - 1, 2)]
        self.nxt, self.prv, self.opp = lax.rem(me + 1, RING), lax.rem(me + RING - 1, RING), lax.rem(me + 2, RING)


class Reduce:
    def __init__(self, copies, ring, acc, bufs):
        self.copies, self.ring, self.acc = copies, ring, acc
        self.pair, self.from_left, self.from_right = bufs

    def begin(self):
        c, r, acc = self.copies, self.ring, self.acc
        self.a1 = c.start(acc(r.opp, 0), self.pair.at[0], r.right)
        self.b1 = c.start(acc(r.opp, 1), self.pair.at[1], r.left)
        self.b2 = c.start(acc(r.nxt, 1), self.from_left.at[1], r.right)
        self.a2 = c.start(acc(r.prv, 0), self.from_right.at[0], r.left)

    def middle(self):
        c, r, acc = self.copies, self.ring, self.acc
        self.a1.wait_recv()
        add = acc(r.nxt, 0)
        add[...] = add[...] + self.pair[0]
        self.a3 = c.start(add, self.from_left.at[0], r.right)
        self.b1.wait_recv()
        add = acc(r.prv, 1)
        add[...] = add[...] + self.pair[1]
        self.b3 = c.start(add, self.from_right.at[1], r.left)

    def end(self, target):
        for copy in (self.b2, self.a3, self.a2, self.b3):
            copy.wait_recv()
        for half in range(2):
            target(half)[...] = self.acc(self.ring.me, half)[...] + self.from_left[half] + self.from_right[half]


class Gather:
    def __init__(self, copies, ring, out):
        self.copies, self.ring, self.out = copies, ring, out

    def send(self, k, half, device):
        return self.copies.start(self.out(k, half), self.out(k, half), device)

    def begin(self):
        r = self.ring
        self.ra = self.send(r.me, 0, r.right)
        self.lb = self.send(r.me, 1, r.left)
        self.rb = self.send(r.me, 1, r.right)
        self.la = self.send(r.me, 0, r.left)

    def relay(self):
        r = self.ring
        self.ra.wait_recv()
        self.ra2 = self.send(r.prv, 0, r.right)
        self.lb.wait_recv()
        self.lb2 = self.send(r.nxt, 1, r.left)
        self.rb.wait_recv()
        self.la.wait_recv()

    def finish(self):
        self.ra2.wait_recv()
        self.lb2.wait_recv()


class Swap:
    def __init__(self, copies, ring, acc, bufs):
        self.copies, self.ring, self.acc, self.bufs = copies, ring, acc, bufs

    def begin(self):
        r = self.ring
        sends = ((r.nxt, r.right), (r.prv, r.left), (r.opp, r.across))
        self.sent = [self.copies.start(self.acc(k), buf, device) for (k, device), buf in zip(sends, self.bufs)]

    def end(self, target):
        for copy in self.sent:
            copy.wait_recv()
        target[...] = (self.acc(self.ring.me)[...] + self.bufs[0][...]) + (self.bufs[1][...] + self.bufs[2][...])


class Spread:
    def __init__(self, copies, ring, out):
        self.copies, self.ring, self.out = copies, ring, out

    def begin(self):
        r = self.ring
        self.sent = [self.copies.start(self.out(r.me), self.out(r.me), device) for device in (r.right, r.left, r.across)]

    def finish(self):
        for copy in self.sent:
            copy.wait_recv()


def rows_of(start, size):
    return pl.ds(pl.multiple_of(start, SUB), size)


def combine_kernel(n_seq, order_hbm, place_hbm, frames_hbm, pred_hbm, w_enc_hbm, w_pred_hbm, da_ref, dc_ref, gw_ref, loss_ref,
                   ge_out, gp_out, gwe_out, gwp_out, gwo_out, loss_out,
                   order_ref, place_ref, frames_ref, pred_ref, w_enc_ref, w_pred_ref, load_sem, dc_out, grad_rows_ref, *scratch):
    sources = (frames_hbm, order_hbm, pred_hbm, w_enc_hbm, place_hbm, w_pred_hbm)
    landed = (frames_ref, order_ref, pred_ref, w_enc_ref, place_ref, w_pred_ref)
    loads = [pltpu.make_async_copy(src, dst, load_sem.at[k]) for k, (src, dst) in enumerate(zip(sources, landed))]
    for copy in loads:
        copy.start()
    (enc_acc, enc_pair, enc_mid, enc_y, enc_x, outs_acc, outs_pair, outs_mid, outs_1, outs_2, pred_acc, pred_y, rows_ref, ge_ref, send_sem, recv_sem) = unflatten(scratch)
    seq = lax.axis_index("seq")
    y = lax.axis_index("data")
    x = lax.div(seq, CORES)
    core = lax.rem(seq, CORES)
    mate = {"seq": x * CORES + 1 - core}
    ring_x = Ring(x, lambda k: {"seq": k * CORES + core})
    ring_y = Ring(y, lambda k: {"data": k})
    barrier = pltpu.get_barrier_semaphore()
    for hop in range(1, n_seq):
        pl.semaphore_signal(barrier, inc=1, device_id={"seq": lax.rem(seq + hop, n_seq)}, device_id_type=MESH)
    for dev in (ring_y.right, ring_y.left, ring_y.across):
        pl.semaphore_signal(barrier, inc=1, device_id=dev, device_id_type=MESH)

    n_blk = gw_ref.shape[0] // 2
    n_utt = n_seq * frames_ref.shape[1]
    n_upos = pred_ref.shape[1]
    enc_half = enc_acc.shape[0] // CORES
    out_half = gw_ref.shape[1] // CORES
    enc_q, out_q = enc_half // RING, out_half // RING
    enc_s = enc_q // RING
    enc_row, out_row = core * enc_half, core * out_half
    contract_rows = (((0,), (0,)), ((), ()))

    n_own = frames_ref.shape[1]
    dc_out[pl.ds(seq * n_own, n_own)] = dc_ref[...].reshape(n_own, n_upos, -1)
    pl.semaphore_wait(barrier, n_seq - 1 + RING - 1)

    copies = Copies(send_sem, recv_sem)

    def swap_out(part):
        blocks = pl.ds(part * n_blk, n_blk)
        return copies.start(gw_ref.at[blocks, rows_of((1 - core) * out_half, out_half), :], outs_pair[part], mate)

    dc_gather = Gather(copies, ring_x, lambda k, half: dc_out.at[pl.ds((k * CORES + core) * n_own + half * (n_own // 2), n_own // 2)])
    swap_1 = swap_out(1)
    dc_gather.begin()
    dc_whole = lambda dev: dc_out.at[pl.ds(dev * n_own, n_own)]
    dc_mate = [copies.start(dc_whole(seq), dc_whole(seq), mate)]
    loads[0].wait()
    frames = frames_ref[...]
    enc_acc[...] = lax.dot_general(frames.reshape(-1, frames.shape[-1]), da_ref[...], contract_rows, preferred_element_type=F32)
    swap_enc = copies.start(enc_acc.at[rows_of((1 - core) * enc_half, enc_half), :], enc_pair, mate)
    swap_0 = swap_out(0)

    def dc_pass(k):
        dc_mate.append(copies.start(dc_whole(k * CORES + core), dc_whole(k * CORES + core), mate))

    def add_out(part):
        outs_acc[part][...] = gw_ref[pl.ds(part * n_blk, n_blk), rows_of(out_row, out_half), :] + outs_pair[part][...]

    def out_first(part):
        return lambda k, half: outs_acc[part].at[:, rows_of(k * out_q + half * (out_q // 2), out_q // 2), :]

    def out_second(part):
        return lambda k: outs_mid[part].at[k]

    rings = ((ring_x, ring_y), (ring_y, ring_x))
    first = [Reduce(copies, rings[part][0], out_first(part), outs_1[part]) for part in range(2)]
    second = [Swap(copies, rings[part][1], out_second(part), outs_2[part]) for part in range(2)]
    enc_first = Reduce(copies, ring_y, lambda k, half: enc_acc.at[rows_of(enc_row + k * enc_q + half * (enc_q // 2), enc_q // 2), :], enc_y)
    enc_second = Swap(copies, ring_x, lambda k: enc_mid.at[rows_of(k * enc_s, enc_s), :], enc_x)
    pred_first = Swap(copies, ring_y, lambda k: pred_acc.at[rows_of(k * enc_s, enc_s), :], pred_y)

    def out_place(part, k1, k2, half, whole=False):
        start, size = out_row + k1 * out_q, out_q
        if not whole:
            start, size = start + half * (out_q // 2), out_q // 2
        return gwo_out.at[part * n_blk + k2 if k2 is not None else pl.ds(part * n_blk, n_blk), rows_of(start, size), :]

    def pair_place(part):
        ring1, ring2 = rings[part]
        return (
            Spread(copies, ring2, lambda k: out_place(part, ring1.me, k, 0, True)),
            Gather(copies, ring1, lambda k, half: out_place(part, k, None, half)),
        )

    a_g1, a_g2 = pair_place(0)
    b_g1, b_g2 = pair_place(1)
    enc_at = lambda k: gwe_out.at[rows_of(enc_row + y * enc_q + k * enc_s, enc_s), :]
    enc_g1 = Spread(copies, ring_x, enc_at)
    enc_g2 = Gather(copies, ring_y, lambda k, half: gwe_out.at[rows_of(enc_row + k * enc_q + half * (enc_q // 2), enc_q // 2), :])
    pred_at = lambda k: gwp_out.at[x, core, rows_of(k * enc_s, enc_s), :]
    pred_g1 = Spread(copies, ring_y, pred_at)
    pred_g2 = Gather(copies, ring_x, lambda k, half: gwp_out.at[k, core, pl.ds(half * (enc_q // 2), enc_q // 2), :])

    last = []

    def pass_on(ref):
        last.append(copies.start(ref, ref, mate))

    a_whole = lambda k: out_place(0, k, None, 0, True)
    b_whole = lambda k: out_place(1, k, None, 0, True)
    enc_whole = lambda k: gwe_out.at[rows_of(enc_row + k * enc_q, enc_q), :]
    pred_whole = lambda k: gwp_out.at[k, core]

    def widen(g1, g2, whole):
        g1.finish()
        g2.begin()
        pass_on(whole(g2.ring.me))

    def relay(g2, whole):
        g2.relay()
        pass_on(whole(g2.ring.prv))
        pass_on(whole(g2.ring.nxt))

    def close(g2, whole):
        g2.finish()
        pass_on(whole(g2.ring.opp))

    swap_1.wait_recv()
    add_out(1)
    first[1].begin()
    swap_enc.wait_recv()
    enc_acc[rows_of(enc_row, enc_half), :] = enc_acc[rows_of(enc_row, enc_half), :] + enc_pair[...]
    dc_gather.relay()
    dc_pass(ring_x.prv)
    dc_pass(ring_x.nxt)
    swap_0.wait_recv()
    add_out(0)
    first[0].begin()
    first[1].middle()
    enc_first.begin()

    loads[3].wait()
    ge = lax.dot_general(da_ref[...], w_enc_ref[...], (((1,), (1,)), ((), ())), preferred_element_type=F32)
    ge_ref[...] = ge.astype(BF16).reshape(ge_ref.shape)
    ge_out[pl.ds(seq, 1)] = ge_ref[pl.ds(seq, 1)]
    loss_out[pl.ds(seq, 1)] = loss_ref[...][None]
    loads[1].wait()
    loads[2].wait()
    for k in range(n_utt):
        rows_ref[k * n_upos:(k + 1) * n_upos, :] = pred_ref[order_ref[k], :, pl.ds(pl.multiple_of(x * LANES, LANES), LANES)]
    dc_gather.finish()
    dc_pass(ring_x.opp)
    first[0].middle()
    first[1].end(lambda half: outs_mid[1].at[:, pl.ds(half * (out_q // 2), out_q // 2), :])
    second[1].begin()

    for copy in dc_mate:
        copy.wait_recv()
    pred_part = lax.dot_general(rows_ref[...], dc_out[...].reshape(n_utt * n_upos, -1), contract_rows, preferred_element_type=F32)
    pred_acc[...] = jnp.where(core == 0, pred_part[:enc_q], pred_part[enc_q:])
    pred_first.begin()
    enc_first.middle()
    small = []
    for hop in range(1, n_seq):
        peer = lax.rem(seq + hop, n_seq)
        small.append(copies.start(ge_ref.at[peer], ge_out.at[seq], {"seq": peer}))
        small.append(copies.start(loss_ref, loss_out.at[seq], {"seq": peer}))
    first[0].end(lambda half: outs_mid[0].at[:, pl.ds(half * (out_q // 2), out_q // 2), :])
    second[0].begin()
    second[1].end(out_place(1, y, x, 0, True))
    b_g1.begin()
    enc_first.end(lambda half: enc_mid.at[pl.ds(half * (enc_q // 2), enc_q // 2), :])
    enc_second.begin()
    pred_first.end(pred_at(y))
    pred_g1.begin()
    second[0].end(out_place(0, x, y, 0, True))
    a_g1.begin()

    loads[4].wait()
    loads[5].wait()
    for i in range(n_utt):
        grad_rows_ref[i] = dc_out[place_ref[i]]
    widen(b_g1, b_g2, b_whole)
    enc_second.end(enc_at(x))
    enc_g1.begin()
    widen(pred_g1, pred_g2, pred_whole)
    half_utt = n_utt // 2

    def grad_rows(part):
        rows = grad_rows_ref[part * half_utt:(part + 1) * half_utt].reshape(half_utt * n_upos, -1)
        grads = lax.dot_general(rows, w_pred_ref[...], (((1,), (1,)), ((), ())), preferred_element_type=F32)
        gp_out[part * half_utt:(part + 1) * half_utt] = grads.reshape(half_utt, n_upos, -1)

    grad_rows(0)
    relay(b_g2, b_whole)
    widen(enc_g1, enc_g2, enc_whole)
    grad_rows(1)
    relay(pred_g2, pred_whole)
    widen(a_g1, a_g2, a_whole)
    close(b_g2, b_whole)
    relay(enc_g2, enc_whole)
    relay(a_g2, a_whole)
    close(pred_g2, pred_whole)
    close(enc_g2, enc_whole)
    close(a_g2, a_whole)
    for copy in small + last:
        copy.wait_recv()
    copies.drain()


N_COPIES = 3 + 10 + 14 + 3 * 6 + 4 * 6 + 4 * 6 + 16


def unflatten(refs):
    refs = list(refs)
    take = lambda n: [refs.pop(0) for _ in range(n)]
    enc_acc, enc_pair, enc_mid = take(3)
    enc_y, enc_x = take(3), take(3)
    outs = [(take(1)[0], take(1)[0], take(1)[0], take(3), take(3)) for _ in range(2)]
    outs_acc, outs_pair, outs_mid, outs_1, outs_2 = zip(*outs)
    pred_acc = refs.pop(0)
    pred_y = take(3)
    return (enc_acc, enc_pair, enc_mid, enc_y, enc_x, outs_acc, outs_pair, outs_mid, outs_1, outs_2, pred_acc, pred_y, *refs)


def combine(n_seq, order, place, frames, pred_loc, w_enc, w_pred, da, dc, gw, loss):
    width = frames.shape[-1]
    n_utt, n_upos, _ = pred_loc.shape
    joint = da.shape[-1]
    n_blk = gw.shape[0] // 2
    enc_half, out_half = width // CORES, joint // CORES
    enc_q, out_q = enc_half // RING, out_half // RING
    enc_s = enc_q // RING
    ring = lambda *shape: [VMEM(shape, F32)] * 3
    outs = [VMEM((n_blk, out_half, LANES), F32)] * 2 + [VMEM((n_blk, out_q, LANES), F32)] + ring(2, n_blk, out_q // 2, LANES) + ring(out_q, LANES)
    return pl.pallas_call(
        functools.partial(combine_kernel, n_seq),
        out_shape=(
            VMEM(frames.shape, BF16),
            VMEM((n_utt, n_upos, width), F32),
            VMEM((width, joint), F32),
            VMEM((RING, CORES, enc_q, joint), F32),
            VMEM(gw.shape, F32),
            VMEM((n_seq,) + loss.shape, F32),
        ),
        in_specs=[pl.BlockSpec(memory_space=pltpu.HBM)] * 6 + [vspec()] * 4,
        out_specs=(vspec(),) * 6,
        scratch_shapes=[pltpu.SMEM(order.shape, jnp.int32)] * 2
        + [VMEM(v.shape, v.dtype) for v in (frames, pred_loc, w_enc, w_pred)]
        + [pltpu.SemaphoreType.DMA((6,)), VMEM((n_utt, n_upos, joint), BF16), VMEM((n_utt, n_upos, joint), BF16)]
        + [VMEM((width, joint), F32), VMEM((enc_half, joint), F32), VMEM((enc_q, joint), F32)]
        + ring(2, enc_q // 2, joint)
        + ring(enc_s, joint)
        + outs
        + outs
        + [VMEM((enc_q, joint), F32)]
        + ring(enc_s, joint)
        + [
            VMEM((n_utt * n_upos, LANES), BF16),
            VMEM(frames.shape, BF16),
            pltpu.SemaphoreType.DMA((N_COPIES,)),
            pltpu.SemaphoreType.DMA((N_COPIES,)),
        ],
        compiler_params=pltpu.CompilerParams(collective_id=1, has_side_effects=True, vmem_limit_bytes=48_000_000),
        name="combine",
    )(*(in_hbm(v) for v in (order, place, frames, pred_loc, w_enc, w_pred)), *(in_vmem(v) for v in (da, dc, gw, loss)))


def output_kernel(place_hbm, losses_ref, ge_ref, gp_ref, gwe_ref, gwp_ref, gw_ref,
                  loss_out, ge_out, gp_out, gwe_out, gwp_out, gwo_out, place_ref, rows_ref, loss_ref, load_sem, sem):
    n_utt = gp_out.shape[0]
    n_own = ge_ref.shape[1]
    n_cols, _, col = gw_ref.shape
    loads = [pltpu.make_async_copy(place_hbm, place_ref, load_sem.at[0]), pltpu.make_async_copy(losses_ref.at[:, 0, :], rows_ref, load_sem.at[1])]
    for copy in loads:
        copy.start()
    pairs = [(gp_ref, gp_out), (gwe_ref, gwe_out)]
    pairs += [(gw_ref.at[k], gwo_out.at[:, pl.ds(k * col, col)]) for k in range(n_cols)]
    blocks, cores, size, _ = gwp_ref.shape
    pairs += [(gwp_ref.at[k // cores, k % cores], gwp_out.at[pl.ds(k * size, size), :]) for k in range(blocks * cores)]
    copies = [pltpu.make_async_copy(src, dst, sem.at[k]) for k, (src, dst) in enumerate(pairs)]
    for copy in copies:
        copy.start()
    for copy in loads:
        copy.wait()
    for i in range(n_utt):
        place = place_ref[i]
        dev = place // n_own
        own = place - dev * n_own
        loss_ref[i] = rows_ref[dev, own]
        copy = pltpu.make_async_copy(ge_ref.at[dev, own], ge_out.at[i], sem.at[len(copies)])
        copy.start()
        copies.append(copy)
    copy = pltpu.make_async_copy(loss_ref, loss_out, sem.at[len(copies)])
    copy.start()
    copies.append(copy)
    for copy in copies:
        copy.wait()


def outputs(place, losses, ge, gp, gwe, gwp, gw):
    n_seq, n_own, t_loc, width = ge.shape
    n_cols, joint, col = gw.shape
    hbm = pl.BlockSpec(memory_space=pltpu.HBM)
    return pl.pallas_call(
        output_kernel,
        out_shape=(
            jax.ShapeDtypeStruct((n_seq * n_own,), F32),
            jax.ShapeDtypeStruct((n_seq * n_own, t_loc, width), BF16),
            jax.ShapeDtypeStruct(gp.shape, F32),
            jax.ShapeDtypeStruct((width, joint), F32),
            jax.ShapeDtypeStruct((width, joint), F32),
            jax.ShapeDtypeStruct((joint, n_cols * col), F32),
        ),
        in_specs=[hbm] + [vspec()] * 6,
        out_specs=(hbm,) * 6,
        scratch_shapes=[
            pltpu.SMEM(place.shape, jnp.int32),
            pltpu.SMEM((n_seq, losses.shape[-1]), F32),
            pltpu.SMEM(place.shape, F32),
            pltpu.SemaphoreType.DMA((2,)),
            pltpu.SemaphoreType.DMA((2 + n_cols + RING * CORES + n_seq * n_own + 1,)),
        ],
        compiler_params=pltpu.CompilerParams(vmem_limit_bytes=48_000_000),
        name="outputs",
    )(in_hbm(place), *(in_vmem(v) for v in (losses, ge, gp, gwe, gwp, gw)))


def solution(mesh):
    n_seq = mesh.shape["seq"]
    utt_rows = P(("part", "data"))
    utt_mats = P(("part", "data"), None)
    utt_cube = P(("part", "data"), None, None)
    enc_spec = P(("part", "data"), "seq", None)
    weight_in = P(None, None)
    weight_out = P("part", None)

    def body(enc_loc, pred_loc, w_enc, w_pred, w_out, labels, frame_len, label_len):
        t_loc = enc_loc.shape[1]
        n_upos = pred_loc.shape[1]
        seq_idx = lax.axis_index("seq").astype(jnp.int32).reshape(1)
        order, place, frames, act, pred, w_out_t = exchange(n_seq, frame_len, label_len, enc_loc, pred_loc, w_enc, w_pred, w_out)
        da, dc, gw, loss = lattice(n_seq, seq_idx, order, frame_len, label_len, labels, act, pred, w_out, w_out_t, n_upos, t_loc)
        ge, gp, gwe, gwp, gw, losses = combine(n_seq, order, place, frames, pred_loc, w_enc, w_pred, da, dc, gw, loss)
        loss, grad_enc, grad_pred, gw_enc, gw_pred, gw_out = outputs(place, losses, ge, gp, gwe, gwp, gw)
        return loss, grad_enc, grad_pred, gw_enc, gw_pred, gw_out

    return jax.shard_map(body, mesh=mesh, in_specs=(enc_spec, utt_cube, weight_in, weight_in, weight_in, utt_mats, utt_rows, utt_rows), out_specs=(utt_rows, enc_spec, utt_cube, weight_out, weight_out, weight_out), check_vma=False)
```

profile of v0, /device:TPU:97, one launch (start us, length us, event | category | flops | bytes accessed | tf_op | source)
XLA Modules:
  0.0 105.8 jit_solution(2599925716282245128)
XLA Ops:
  0.6 13.2 %exchange.1 = (s32[32]{0:T(128)}, s32[32]{0:T(128)}, bf16[8,4,8,512]{3,2,1,0:T(8,128)(2,1)}, f32[256,640]{1,0:T(8,128)S(1)}, f32[128,640]{1,0:T(8,128)S(1)}, /*index=5*/bf16[1024,640]{1,0:T(8,128)(2,1)S(1)}) custom-call(s32[32]{0:T(128)} %flen_ref.1, s32[32]{0:T(128)} %llen_ref.1, bf16[32,8,512]{2,1,0:T(8,128)(2,1)} %enc_hbm.1, ...), custom_call_target="tpu_custom_call" | custom-call | tf_op jit(solution)/shard_map/exchange/pallas_call | solution.py:121
  13.8 41.2 %lattice.1 = (bf16[256,640]{1,0:T(8,128)(2,1)S(1)}, bf16[128,640]{1,0:T(8,128)(2,1)S(1)}, f32[8,640,128]{2,1,0:T(8,128)S(1)}, f32[8,128]{1,0:T(8,128)S(1)}) custom-call(s32[1]{0:T(128)} %bitcast.seq_ref, s32[32]{0:T(128)} %get-tuple-element.23.order_ref.order_hbm, s32[32]{0:T(128)} %flen_ref.1, s32[32]{0:T(128)} %llen_ref.1, s32[32,31]{1,0:T(8,128)} %labels_ref.1, ...), custom_call_target="tpu_custom_call" | custom-call | tf_op jit(solution)/shard_map/lattice/pallas_call | solution.py:409
  55.0 47.2 %combine.1 = (bf16[8,4,8,512]{3,2,1,0:T(8,128)(2,1)S(1)}, f32[32,32,512]{2,1,0:T(8,128)S(1)}, f32[512,640]{1,0:T(8,128)S(1)}, f32[4,2,64,640]{3,2,1,0:T(8,128)S(...) custom-call(s32[32]{0:T(128)} %get-tuple-element.23.order_ref.order_hbm, s32[32]{0:T(128)} %get-tuple-element.22.place_hbm, ...), custom_call_target="tpu_custom_call" | custom-call | tf_op jit(solution)/shard_map/combine/pallas_call | solution.py:779
  102.2 3.5 %outputs.1 = (f32[32]{0:T(128)}, bf16[32,8,512]{2,1,0:T(8,128)(2,1)}, f32[32,32,512]{2,1,0:T(8,128)}, f32[512,640]{1,0:T(8,128)}, f32[512,640]{1,0:T(8,128)}, /*index=5*/f32[640,1024]{1,0:T(8,128)}) custom-call(s32[32]{0:T(128)} %get-tuple-element.22.place_hbm, f32[8,8,128]{2,1,0:T(8,128)S(1)} %get-tuple-element.32.losses_ref, ...), custom_call_target="tpu_custom_call" | custom-call | tf_op jit(solution)/shard_map/outputs/pallas_call | solution.py:848
where the time goes:
time: 106 us
  Pallas kernels  105 us (99%)
    pallas_call x1, Pallas kernels, combine(): pl.pallas_call(functools.partial(combine_kernel, n_seq), out_shape=(VMEM(...  47.2 us
    pallas_call x1, Pallas kernels, lattice(): pl.pallas_call(functools.partial(lattice_kernel, n_own, n_frames, n_upos)...  41.2 us
    pallas_call x1, Pallas kernels, exchange(): pl.pallas_call(functools.partial(exchange_kernel, n_seq), out_shape=(pltp...  13.2 us
    pallas_call x1, Pallas kernels, outputs(): pl.pallas_call(output_kernel, out_shape=(jax.ShapeDtypeStruct((n_seq * n_...  3.53 us

commit v1 on v0

--- a/solution.py
+++ b/solution.py
@@ -40,7 +40,7 @@
 
 def exchange_kernel(n_seq, flen_hbm, llen_hbm, enc_hbm, pred_hbm, w_enc_hbm, w_pred_hbm, w_out_hbm,
                     order_ref, place_ref, frames_ref, a_ref, c_ref, w_out_t_ref,
-                    key_ref, sorted_ref, own_pred_ref, flen_ref, llen_ref, enc_ref, pred_ref, w_enc_ref, w_pred_ref, w_out_ref, load_sem, send_sem, recv_sem):
+                    key_ref, cost_ref, rank_ref, by_rank_ref, sorted_ref, own_pred_ref, flen_ref, llen_ref, enc_ref, pred_ref, w_enc_ref, w_pred_ref, w_out_ref, load_sem, send_sem, recv_sem):
     sources = (flen_hbm, llen_hbm, enc_hbm, pred_hbm, w_pred_hbm, w_out_hbm, w_enc_hbm)
     landed = (flen_ref, llen_ref, enc_ref, pred_ref, w_pred_ref, w_out_ref, w_enc_ref)
     loads = [pltpu.make_async_copy(src, dst, load_sem.at[k]) for k, (src, dst) in enumerate(zip(sources, landed))]
@@ -54,32 +54,48 @@
         pl.semaphore_signal(barrier, inc=1, device_id={"seq": lax.rem(seq + hop, n_seq)}, device_id_type=MESH)
 
     def set_key(i, carry):
-        key_ref[i] = ((flen_ref[i] + SUB - 1) // SUB) * ((llen_ref[i] + SUB) // SUB) * n_utt + i
+        cost = ((flen_ref[i] + SUB - 1) // SUB) * ((llen_ref[i] + SUB) // SUB)
+        cost_ref[i] = cost
+        key_ref[i] = cost * n_utt + i
         return carry
 
-    def set_place(i, carry):
+    def set_rank(i, carry):
         key = key_ref[i]
         rank = jnp.int32(0)
         for j in range(n_utt):
             rank = rank + jnp.where(key_ref[j] > key, 1, 0)
-        deal = rank // n_seq
-        at = rank - deal * n_seq
-        at = jnp.where(deal % 2 == 0, at, n_seq - 1 - at)
-        place_ref[i] = at * n_own + deal
+        rank_ref[i] = rank
         return carry
 
-    def set_order(k, carry):
-        utt = jnp.int32(0)
-        for j in range(n_utt):
-            utt = utt + jnp.where(place_ref[j] == k, j, 0)
-        order_ref[k] = utt
-        return carry
+    def invert(src_ref, dst_ref):
+        def body(k, carry):
+            found = jnp.int32(0)
+            for j in range(n_utt):
+                found = found + jnp.where(src_ref[j] == k, j, 0)
+            dst_ref[k] = found
+            return carry
+
+        lax.fori_loop(0, n_utt, body, 0)
 
     loads[0].wait()
     loads[1].wait()
     lax.fori_loop(0, n_utt, set_key, 0)
-    lax.fori_loop(0, n_utt, set_place, 0)
-    lax.fori_loop(0, n_utt, set_order, 0)
+    lax.fori_loop(0, n_utt, set_rank, 0)
+    invert(rank_ref, by_rank_ref)
+    sums = [jnp.int32(0)] * n_seq
+    for deal in range(n_own):
+        spots = []
+        for d in range(n_seq):
+            spot = jnp.int32(0)
+            for e in range(n_seq):
+                if e != d:
+                    before = sums[e] <= sums[d] if e < d else sums[e] < sums[d]
+                    spot = spot + jnp.where(before, 1, 0)
+            spots.append(spot)
+        for d in range(n_seq):
+            utt = by_rank_ref[deal * n_seq + spots[d]]
+            order_ref[d * n_own + deal] = utt
+            sums[d] = sums[d] + cost_ref[utt]
     loads[2].wait()
     for k in range(n_utt):
         sorted_ref[k] = enc_ref[order_ref[k]]
@@ -106,6 +122,7 @@
     c_ref[...] = jnp.dot(own_pred.reshape(-1, own_pred.shape[-1]), w_pred_ref[...], preferred_element_type=F32).astype(BF16).astype(F32)
     loads[5].wait()
     w_out_t_ref[...] = w_out_ref[...].T
+    invert(order_ref, place_ref)
     loads[6].wait()
     for copy in copies:
         copy.wait()
@@ -131,6 +148,9 @@
         in_specs=[pl.BlockSpec(memory_space=pltpu.HBM)] * 7,
         out_specs=(sspec(),) * 2 + (vspec(),) * 4,
         scratch_shapes=[
+            pltpu.SMEM((n_utt,), jnp.int32),
+            pltpu.SMEM((n_utt,), jnp.int32),
+            pltpu.SMEM((n_utt,), jnp.int32),
             pltpu.SMEM((n_utt,), jnp.int32),
             VMEM(enc_loc.shape, BF16),
             VMEM((n_own, n_upos, width), BF16),
@@ -271,7 +291,12 @@
             make_hidden(i + 2)
         return carry
 
-    lax.fori_loop(0, lax.div(n_tiles + 1, 2), forward, 0)
+    def forward_tail(_, carry):
+        make_softmax(n_tiles - 1, work0)
+        return carry
+
+    lax.fori_loop(0, lax.div(n_tiles, 2), forward, 0)
+    lax.fori_loop(0, lax.rem(n_tiles, 2), forward_tail, 0)
 
     upos = lax.broadcasted_iota(jnp.int32, (n_upos, LANES), 0)
     utt = lax.broadcasted_iota(jnp.int32, (n_upos, LANES), 1)
@@ -371,30 +396,32 @@
                 cube = [jnp.where(low, cube[k], cube[k + half]) + jnp.where(low, pltpu.roll(cube[k], SUB - shift, 0), pltpu.roll(cube[k + half], shift, 0)) for k in range(half)]
             dact_ref[act_row(b, ti), cols] += cube[0]
 
-    wide_rows = WIDE * rows_g
-    n_wide = lax.div(total + WIDE - 1, WIDE)
-
-    def clear(i, carry):
-        h_ref[pl.ds(pl.multiple_of(i * rows_t, rows_t), rows_t), :] = jnp.zeros((rows_t, joint), BF16)
-        return carry
-
-    lax.fori_loop(n_tiles, n_wide * (WIDE // GROUPS), clear, 0)
-
-    def backward(i, carry):
-        groups = [(i * WIDE + g, g, *decode(i * WIDE + g)) for g in range(WIDE)]
+    def backward_tile(start, width):
+        groups = [(start + g, g, *decode(start + g)) for g in range(width)]
+        rows = width * rows_g
         for group in groups:
             make_dz(*group)
-        dh_ref[...] = jnp.dot(dz_ref[...], wt_ref[...], preferred_element_type=F32)
-        h = h_ref[pl.ds(pl.multiple_of(i * wide_rows, wide_rows), wide_rows), :]
+        dh_ref[:rows] = jnp.dot(dz_ref[:rows], wt_ref[...], preferred_element_type=F32)
+        h = h_ref[pl.ds(pl.multiple_of(start * rows_g, GROUPS * rows_g), rows), :]
         for v in range(0, n_vt, 2):
-            part = lax.dot_general(h, dz_ref[:, v * LANES:(v + 2) * LANES], (((0,), (0,)), ((), ())), preferred_element_type=F32)
+            part = lax.dot_general(h, dz_ref[:rows, v * LANES:(v + 2) * LANES], (((0,), (0,)), ((), ())), preferred_element_type=F32)
             gw_ref[v] += part[:, :LANES]
             gw_ref[v + 1] += part[:, LANES:]
         for group in groups:
             make_sums(*group[1:])
+
+    def backward(i, carry):
+        backward_tile(i * WIDE, WIDE)
         return carry
 
+    n_wide = lax.div(total + WIDE - GROUPS - 1, WIDE)
+
+    def backward_tail(_, carry):
+        backward_tile(n_wide * WIDE, GROUPS)
+        return carry
+
     lax.fori_loop(0, n_wide, backward, 0)
+    lax.fori_loop(0, jnp.where(total > n_wide * WIDE, 1, 0), backward_tail, 0)
     da_ref[...] = dact_ref[...].astype(BF16)
     dc_ref[...] = dpred_ref[...].astype(BF16)
 

time: 106 us -> 106 us (level)
    pallas_call x1, Pallas kernels: 41.2 us -> 39.5 us  [lattice(): pl.pallas_call(functools.partial(lattice_kernel, n_own, n_frames, n_upos)...]
    pallas_call x1, Pallas kernels: 47.2 us -> 48.8 us  [combine(): pl.pallas_call(functools.partial(combine_kernel, n_seq), out_shape=(VMEM(...]
where the time goes in v1:
time: 106 us
  Pallas kernels  105 us (99%)
    pallas_call x1, Pallas kernels, combine(): pl.pallas_call(functools.partial(combine_kernel, n_seq), out_shape=(VMEM(...  48.8 us
    pallas_call x1, Pallas kernels, lattice(): pl.pallas_call(functools.partial(lattice_kernel, n_own, n_frames, n_upos)...  39.5 us
    pallas_call x1, Pallas kernels, exchange(): pl.pallas_call(functools.partial(exchange_kernel, n_seq), out_shape=(pltp...  13.2 us
    pallas_call x1, Pallas kernels, outputs(): pl.pallas_call(output_kernel, out_shape=(jax.ShapeDtypeStruct((n_seq * n_...  3.53 us

profile of v1, /device:TPU:97, one launch (start us, length us, event | category | flops | bytes accessed | tf_op | source)
XLA Modules:
  0.0 105.8 jit_solution(1291520979772114371)
XLA Ops:
  0.6 13.2 %exchange.1 = (s32[32]{0:T(128)}, s32[32]{0:T(128)}, bf16[8,4,8,512]{3,2,1,0:T(8,128)(2,1)}, f32[256,640]{1,0:T(8,128)S(1)}, f32[128,640]{1,0:T(8,128)S(1)}, /*index=5*/bf16[1024,640]{1,0:T(8,128)(2,1)S(1)}) custom-call(s32[32]{0:T(128)} %flen_ref.1, s32[32]{0:T(128)} %llen_ref.1, bf16[32,8,512]{2,1,0:T(8,128)(2,1)} %enc_hbm.1, ...), custom_call_target="tpu_custom_call" | custom-call | tf_op jit(solution)/shard_map/exchange/pallas_call | solution.py:138
  13.9 39.5 %lattice.1 = (bf16[256,640]{1,0:T(8,128)(2,1)S(1)}, bf16[128,640]{1,0:T(8,128)(2,1)S(1)}, f32[8,640,128]{2,1,0:T(8,128)S(1)}, f32[8,128]{1,0:T(8,128)S(1)}) custom-call(s32[1]{0:T(128)} %bitcast.seq_ref, s32[32]{0:T(128)} %get-tuple-element.23.order_ref.order_hbm, s32[32]{0:T(128)} %flen_ref.1, s32[32]{0:T(128)} %llen_ref.1, s32[32,31]{1,0:T(8,128)} %labels_ref.1, ...), custom_call_target="tpu_custom_call" | custom-call | tf_op jit(solution)/shard_map/lattice/pallas_call | solution.py:436
  53.3 48.8 %combine.1 = (bf16[8,4,8,512]{3,2,1,0:T(8,128)(2,1)S(1)}, f32[32,32,512]{2,1,0:T(8,128)S(1)}, f32[512,640]{1,0:T(8,128)S(1)}, f32[4,2,64,640]{3,2,1,0:T(8,128)S(...) custom-call(s32[32]{0:T(128)} %get-tuple-element.23.order_ref.order_hbm, s32[32]{0:T(128)} %get-tuple-element.22.place_hbm, ...), custom_call_target="tpu_custom_call" | custom-call | tf_op jit(solution)/shard_map/combine/pallas_call | solution.py:806
  102.1 3.5 %outputs.1 = (f32[32]{0:T(128)}, bf16[32,8,512]{2,1,0:T(8,128)(2,1)}, f32[32,32,512]{2,1,0:T(8,128)}, f32[512,640]{1,0:T(8,128)}, f32[512,640]{1,0:T(8,128)}, /*index=5*/f32[640,1024]{1,0:T(8,128)}) custom-call(s32[32]{0:T(128)} %get-tuple-element.22.place_hbm, f32[8,8,128]{2,1,0:T(8,128)S(1)} %get-tuple-element.32.losses_ref, ...), custom_call_target="tpu_custom_call" | custom-call | tf_op jit(solution)/shard_map/outputs/pallas_call | solution.py:875
